TPU v7x, 256 devices: a whole 4x4x8 slice. The times are simulated.
256 devices in a mesh: seq: 64 (over y, z, x_hi), tp: 4 (over x_lo, core).
Axes of the slice: x: 4 (x_hi: 2, x_lo: 2; x = x_hi * 2 + x_lo), y: 4, z: 8, core: 2. Of those that a mesh axis runs over, the one named last changes fastest.
Arguments:
- inputs: bfloat16 [8192, 2048], P(('seq', 'tp')), may hold values from -40 to 40
- gain: float32 [2048], replicated, may hold values from 0.5 to 1.5
- w_gate: bfloat16 [2048, 7168], P('seq', 'tp'), may hold values from -0.125 to 0.125
- w_up: bfloat16 [2048, 7168], P('seq', 'tp'), may hold values from -0.125 to 0.125
- grad_act: bfloat16 [8192, 7168], P('seq', 'tp'), may hold values from -12 to 12
Outputs:
- input_grad: bfloat16 [8192, 2048], P(('seq', 'tp'))
- gain_grad: float32 [2048], replicated
- gate_weight_grad: float32 [2048, 7168], P('seq', 'tp')
All inputs are finite; a program needn't handle non-finite values.
Results may differ from a plain program's by a relative error of at most 0.012.
Values may be sent and summed in bfloat16 or wider, within the bound.
No kernel may reach another device: no remote copies, remote signals or barrier semaphores. Data moves between devices by JAX's collectives and lax.ppermute only.
A program may use at most 128 MiB of HBM per device.

v0:
```python
import jax
import jax.numpy as jnp
from jax import lax
from jax.sharding import Mesh
from jax.sharding import PartitionSpec as P

TP = ("tp_0", "tp_1")
SEQ = ("seq_0", "seq_1", "seq_2")
SEQ_TP = ("seq_0", "seq_1", "seq_2", "tp_0", "tp_1")


def sent_to_all(value, axis):
    peers = lax.axis_size(axis)
    return lax.all_to_all(
        jnp.broadcast_to(value[None], (peers, *value.shape)), axis, 0, 0, tiled=True
    )


def laid_out(parts, dim):
    dims = list(parts.shape[1:])
    dims[dim] *= parts.shape[0]
    return jnp.moveaxis(parts, 0, dim).reshape(dims)


def collect(value, axis, dim):
    parts = sent_to_all(value, axis)
    return laid_out(parts, dim)


def in_one_piece(arrays, axis, dim, along):
    widths = [a.shape[along] for a in arrays]
    both = jnp.concatenate(arrays, axis=along)
    out = lax.all_gather(both, axis, axis=dim, tiled=True)
    return tuple(jnp.split(out, [sum(widths[:k]) for k in range(1, len(widths))], axis=along))


def split_up(value, dim, peers):
    dims = value.shape
    parts = value.reshape(*dims[:dim], peers, dims[dim] // peers, *dims[dim + 1 :])
    return jnp.moveaxis(parts, dim, 0)


def sum_at_owner(value, axis, dim):
    parts = split_up(value, dim, lax.axis_size(axis))
    arrived = lax.all_to_all(parts, axis, split_axis=0, concat_axis=0, tiled=True)
    return arrived.astype(jnp.float32).sum(axis=0)


def over_axes(value, axes):
    for axis in axes:
        value = lax.psum(value, axis)
    return value


def own_rows_2(terms, axes):
    so_far = terms.astype(jnp.bfloat16)
    for axis in axes:
        so_far = lax.psum_scatter(so_far, axis, scatter_dimension=0, tiled=True)
    return so_far.astype(jnp.float32)


def on_device(inputs, gain, w_gate, w_up, grad_act):
    group_inputs = collect(inputs, TP, 0)
    values = group_inputs.astype(jnp.float32)
    inverse = lax.rsqrt(jnp.mean(values * values, axis=-1, keepdims=True) + 1e-05)
    scaled = values * inverse
    normed = (scaled * gain).astype(jnp.bfloat16)
    full_gate, full_up = in_one_piece((w_gate, w_up), SEQ, 0, 1)
    gate = jnp.dot(normed, full_gate, preferred_element_type=jnp.float32)
    up = jnp.dot(normed, full_up, preferred_element_type=jnp.float32)
    sigmoid_gate = jax.nn.sigmoid(gate)
    cotangent = grad_act.astype(jnp.float32)
    d_up = (cotangent * gate * sigmoid_gate).astype(jnp.bfloat16)
    d_gate = (cotangent * up * sigmoid_gate * (1.0 + gate * (1.0 - sigmoid_gate))).astype(
        jnp.bfloat16
    )
    contract = (((1,), (1,)), ((), ()))
    partial_grad = lax.dot_general(d_gate, full_gate, contract, preferred_element_type=jnp.float32)
    partial_grad = partial_grad + lax.dot_general(
        d_up, full_up, contract, preferred_element_type=jnp.float32
    )
    own_grad = sum_at_owner(partial_grad.astype(jnp.bfloat16), TP, 0)
    own_rows = own_grad.shape[0]
    offset = lax.axis_index(TP) * own_rows
    own_scaled = lax.dynamic_slice_in_dim(scaled, offset, own_rows, 0)
    own_inverse = lax.dynamic_slice_in_dim(inverse, offset, own_rows, 0)
    gain_grad = over_axes(jnp.sum(own_grad * own_scaled, axis=0), SEQ_TP)
    gained = own_grad * gain
    middle = jnp.mean(gained * own_scaled, axis=-1, keepdims=True)
    input_grad = (own_inverse * (gained - own_scaled * middle)).astype(jnp.bfloat16)
    gate_weight_grad = own_rows_2(
        lax.dot_general(
            normed, d_gate, (((0,), (0,)), ((), ())), preferred_element_type=jnp.float32
        ),
        SEQ,
    )
    return (input_grad, gain_grad, gate_weight_grad)


def solution(mesh):
    torus = Mesh(mesh.devices.reshape(4, 8, 2, 2, 2), ("seq_0", "seq_1", "seq_2", "tp_0", "tp_1"))
    placed = (P(SEQ_TP, None), P(), P(SEQ, TP), P(SEQ, TP), P(SEQ, TP))
    return jax.shard_map(
        on_device,
        mesh=torus,
        in_specs=placed,
        out_specs=(P(SEQ_TP, None), P(), P(SEQ, TP)),
        check_vma=False,
    )
```

profile of v0, /device:TPU:1, one launch (start us, length us, event | category | flops | bytes accessed | tf_op | source)
XLA Modules:
  0.0 380.7 jit_solution(14655092618514983426)
XLA Ops:
  7.2 0.0 all-gather.2.cloned.1.call-start
  7.2 1.7 pad_maximum_fusion
  8.9 0.0 all-gather.2.cloned.1.call-update
  8.9 0.0 copy-start.1
  8.9 0.0 reduce-scatter.4.cloned.1.call-start
  9.0 1.0 broadcast_in_dim.2
  10.0 13.4 %all_to_all.10 = bf16[4,32,2048]{2,1,0:T(8,128)(2,1)S(1)} all-to-all(bf16[4,32,2048]{2,1,0:T(8,128)(2,1)S(1)} %broadcast_in_dim.2), channel_id=1, replica_groups=mesh['seq_0'=4,'seq_1'=8,'seq_2'=2,'tp_0'=2,'tp_1'=2] {'tp_0','tp_1'}, dimensions={0} | all-to-all | bytes 1048576 | tf_op jit(solution)/shard_map/all_to_all | solution.py:14
  23.3 0.2 multiply_reduce_fusion
  23.5 0.1 rsqrt.20
  23.6 0.9 bitcast_multiply_fusion
  24.5 184.2 %all-gather.2.cloned.1.call-done = bf16[2048,3584]{1,0:T(8,128)(2,1)} async-done(((bf16[32,3584]{1,0:T(8,128)(2,1)}), bf16[2048,3584]{1,0:T(8,128)(2,1)}) %all-gather.2.cloned.1.call-update) | async-done | bytes 14680080 | tf_op jit(solution)/shard_map/all_gather | solution.py:33
  208.7 4.2 %fusion.2 = f32[128,1792]{1,0:T(8,128)S(1)} fusion(bf16[128,2048]{1,0:T(8,128)(2,1)S(1)} %get-tuple-element.6, bf16[2048,3584]{1,0:T(8,128)(2,1)} %all-gather.2.cloned.1.call-done), kind=kOutput, calls=%fused_computation.3 | convolution fusion | flops 939524096 | bytes 8781824 | tf_op jit(solution)/shard_map/dot_general | solution.py:69
  212.9 0.0 copy-done.1
  212.9 4.5 %fusion.23 = bf16[128,1792]{1,0:T(8,128)(2,1)S(1)} fusion(bf16[128,2048]{1,0:T(8,128)(2,1)S(1)} %get-tuple-element.6, bf16[2048,3584]{1,0:T(8,128)(2,1)} %all-gather.2.cloned.1.call-done, bf16[128,1792]{1,0:T(8,128)(2,1)S(1)} %copy-done.1, f32[128,1792]{1,0:T(8,128)S(1)} %fusion.2), kind=kOutput, calls=%fused_computation.14 | convolution fusion | flops 942047232 | bytes 9699328 | tf_op jit(solution)/shard_map/dot_general | solution.py:70
  217.4 5.0 %convolution_convert_fusion = bf16[2048,1792]{1,0:T(8,128)(2,1)} fusion(bf16[128,2048]{1,0:T(8,128)(2,1)S(1)} %get-tuple-element.6, bf16[128,1792]{1,0:T(8,128)(2,1)S(1)} %fusion.23), kind=kOutput, calls=%fused_computation | convolution fusion | flops 943194112 | bytes 8323072 | tf_op jit(solution)/shard_map/dot_general | solution.py:92
  222.5 0.0 reduce-scatter.4.cloned.1.call-update
  222.5 0.0 reduce-scatter.6.cloned.1.call-start
  222.5 72.7 %reduce-scatter.4.cloned.1.call-done = bf16[512,1792]{1,0:T(8,128)(2,1)} async-done(((bf16[2048,1792]{1,0:T(8,128)(2,1)}), bf16[512,1792]{1,0:T(8,128)(2,1)}) %reduce-scatter.4.cloned.1.call-update) | async-done | bytes 1835024 | tf_op jit(solution)/shard_map/reduce_scatter | solution.py:58
  295.2 0.0 reduce-scatter.6.cloned.1.call-update
  295.3 5.5 %fusion = f32[128,2048]{1,0:T(8,128)S(1)} fusion(bf16[128,1792]{1,0:T(8,128)(2,1)S(1)} %fusion.23, bf16[2048,3584]{1,0:T(8,128)(2,1)} %all-gather.2.cloned.1.call-done), kind=kOutput, calls=%fused_computation.1 | convolution fusion | flops 939524096 | bytes 8847360 | tf_op jit(solution)/shard_map/dot_general | solution.py:78
  300.8 0.0 copy-start
  300.8 6.4 %fusion.20 = bf16[128,2048]{1,0:T(8,128)(2,1)} fusion(f32[128,2048]{1,0:T(8,128)S(1)} %fusion, bf16[2048,3584]{1,0:T(8,128)(2,1)} %all-gather.2.cloned.1.call-done, f32[128,1792]{1,0:T(8,128)S(1)} %fusion.2, bf16[128,1792]{1,0:T(8,128)(2,1)S(1)} %copy-done.1), kind=kOutput, calls=%fused_computation.13 | convolution fusion | flops 941654016 | bytes 10289152 | tf_op jit(solution)/shard_map/dot_general | solution.py:79
  307.2 4.2 %all-to-all-start.1 = ((bf16[4,32,2048]{2,1,0:T(8,128)(2,1)}), bf16[4,32,2048]{2,1,0:T(8,128)(2,1)S(1)}, u32[]{:S(2)}, u32[]{:S(2)}) async-start(bf16[4,32,2048]{2,1,0:T(8,128)(2,1)} %bitcast.2), calls=%async_computation.1 | async-start | bytes 1048576 | tf_op jit(solution)/shard_map/all_to_all | solution.py:45
  311.4 0.0 reduce-scatter.8.cloned.1.call-start
  311.4 0.1 rsqrt.19
  311.5 0.1 dynamic-slice_bitcast_fusion
  311.5 7.7 %all-to-all-done.1 = bf16[4,32,2048]{2,1,0:T(8,128)(2,1)S(1)} async-done(((bf16[4,32,2048]{2,1,0:T(8,128)(2,1)}), bf16[4,32,2048]{2,1,0:T(8,128)(2,1)S(1)}, u32[]{:S(2)}, u32[]{:S(2)}) %all-to-all-start.1) | async-done | bytes 524320 | tf_op jit(solution)/shard_map/all_to_all | solution.py:45
  319.2 0.1 convert_reduce_fusion
  319.3 0.0 copy-done
  319.3 0.2 multiply_reduce_fusion.1
  319.5 7.5 %psum.35 = f32[2048]{0:T(1024)S(1)} all-reduce(f32[2048]{0:T(1024)S(1)} %get-tuple-element.3), channel_id=1, replica_groups=mesh['seq_0'=4,'seq_1'=8,'seq_2'=2,'tp_0'=2,'tp_1'=2] {'seq_0'}, use_global_device_ids=true, to_apply=%region_4.0 | all-reduce | flops 2048 | bytes 16384 | tf_op jit(solution)/shard_map/psum | solution.py:51
  327.0 13.8 %psum.36 = f32[2048]{0:T(1024)S(1)} all-reduce(f32[2048]{0:T(1024)S(1)} %psum.35), channel_id=1, replica_groups=mesh['seq_0'=4,'seq_1'=8,'seq_2'=2,'tp_0'=2,'tp_1'=2] {'seq_1'}, use_global_device_ids=true, to_apply=%region_5.0 | all-reduce | flops 2048 | bytes 16384 | tf_op jit(solution)/shard_map/psum | solution.py:51
  340.8 5.4 %psum.37 = f32[2048]{0:T(1024)S(1)} all-reduce(f32[2048]{0:T(1024)S(1)} %psum.36), channel_id=1, replica_groups=mesh['seq_0'=4,'seq_1'=8,'seq_2'=2,'tp_0'=2,'tp_1'=2] {'seq_2'}, use_global_device_ids=true, to_apply=%region_6.0 | all-reduce | flops 2048 | bytes 16384 | tf_op jit(solution)/shard_map/psum | solution.py:51
  346.2 3.8 %psum.38 = f32[2048]{0:T(1024)S(1)} all-reduce(f32[2048]{0:T(1024)S(1)} %psum.37), channel_id=1, replica_groups=mesh['seq_0'=4,'seq_1'=8,'seq_2'=2,'tp_0'=2,'tp_1'=2] {'tp_0'}, use_global_device_ids=true, to_apply=%region_7.0 | all-reduce | flops 2048 | bytes 16384 | tf_op jit(solution)/shard_map/psum | solution.py:51
  350.0 0.0 reduce-scatter.6.cloned.1.call-done
  350.1 0.0 reduce-scatter.8.cloned.1.call-update
  350.1 11.1 %psum.39 = f32[2048]{0:T(1024)} all-reduce(f32[2048]{0:T(1024)S(1)} %psum.38), channel_id=1, replica_groups=mesh['seq_0'=4,'seq_1'=8,'seq_2'=2,'tp_0'=2,'tp_1'=2] {'tp_1'}, use_global_device_ids=true, to_apply=%region_8.0 | all-reduce | flops 2048 | bytes 16384 | tf_op jit(solution)/shard_map/psum | solution.py:51
  361.1 0.8 multiply_convert_fusion.1
  361.9 10.7 %reduce-scatter.8.cloned.1.call-done = bf16[32,1792]{1,0:T(8,128)(2,1)} async-done(((bf16[64,1792]{1,0:T(8,128)(2,1)}), bf16[32,1792]{1,0:T(8,128)(2,1)}) %reduce-scatter.8.cloned.1.call-update) | async-done | bytes 114704 | tf_op jit(solution)/shard_map/reduce_scatter | solution.py:58
  372.6 1.6 convert_element_type.47
  (2 shorter events, 0.0 us)
Async XLA Ops:
  7.2 201.5 %all-gather.2.cloned.1.call-start = ((), (), s32[]{:S(2)}) async-start(), calls=%async_computation.5 | async-start | bytes 14909440 | tf_op jit(solution)/shard_map/all_gather | solution.py:33
  8.9 204.0 %copy-start.1 = (bf16[128,1792]{1,0:T(8,128)(2,1)S(1)}, bf16[128,1792]{1,0:T(8,128)(2,1)}, u32[]{:S(2)}) copy-start(bf16[128,1792]{1,0:T(8,128)(2,1)} %param.9) | copy-start | bytes 1376260
  8.9 286.3 %reduce-scatter.4.cloned.1.call-start = ((), (), s32[]{:S(2)}) async-start(), calls=%async_computation.6 | async-start | bytes 9175040 | tf_op jit(solution)/shard_map/reduce_scatter | solution.py:58
  222.5 127.6 %reduce-scatter.6.cloned.1.call-start = ((), (), s32[]{:S(2)}) async-start(), calls=%async_computation.7 | async-start | bytes 2064384 | tf_op jit(solution)/shard_map/reduce_scatter | solution.py:58
  300.8 18.5 %copy-start = (f32[2048]{0:T(1024)S(1)}, f32[2048]{0:T(1024)}, u32[]{:S(2)}) copy-start(f32[2048]{0:T(1024)} %param.6) | copy-start | bytes 24580
  307.2 12.0 %all-to-all-start.1 = ((bf16[4,32,2048]{2,1,0:T(8,128)(2,1)}), bf16[4,32,2048]{2,1,0:T(8,128)(2,1)S(1)}, u32[]{:S(2)}, u32[]{:S(2)}) async-start(bf16[4,32,2048]{2,1,0:T(8,128)(2,1)} %bitcast.2), calls=%async_computation.1 | async-start | bytes 1048576 | tf_op jit(solution)/shard_map/all_to_all | solution.py:45
  311.4 61.2 %reduce-scatter.8.cloned.1.call-start = ((), (), s32[]{:S(2)}) async-start(), calls=%async_computation.8 | async-start | bytes 344064 | tf_op jit(solution)/shard_map/reduce_scatter | solution.py:58
Sparse Core Ops, SparseCore 0:
  12.2 196.4 all-gather.1
  222.6 72.5 reduce-scatter.3
  297.8 37.3 reduce-scatter.5
  350.2 22.3 reduce-scatter.7
where the time goes:
time: 381 us
  waiting for transfers between devices  275 us (72%)
  blocking collectives  55 us (14%)
  matrix products  25.7 us (7%)
  between operations  13.9 us (4%)
  other arithmetic  5.36 us (1%)
  starting transfers between devices  4.29 us (1%)
    all_gather x1, waiting for transfers between devices, in_one_piece(): out = lax.all_gather(both, axis, axis=dim, tiled=True)  184 us
    reduce_scatter x3, waiting for transfers between devices, own_rows_2(): so_far = lax.psum_scatter(so_far, axis, scatter_dimension=0, tiled=True)  83.4 us
    psum x5, blocking collectives, over_axes(): value = lax.psum(value, axis)  41.6 us
    all_to_all x1, blocking collectives, sent_to_all(): lax.all_to_all(jnp.broadcast_to(value[None], (peers, *value.shape)), axis...  13.4 us
    all_to_all x1, waiting for transfers between devices, sum_at_owner(): lax.all_to_all(parts, axis, split_axis=0, concat_axis=0, tiled=True)  7.69 us
  transfers between devices with their start and end apart: 5, of which 4 were waited for; matrix products, arithmetic and copies ran while one was open for 4% of the time, Pallas kernels for 0%

commit v1 on v0

--- a/solution.py
+++ b/solution.py
@@ -48,7 +48,8 @@
 
 def over_axes(value, axes):
     for axis in axes:
-        value = lax.psum(value, axis)
+        pieces = lax.all_gather(value, axis)
+        value = jnp.sum(pieces, axis=0)
     return value
 
 

time: 381 us -> 393 us (1.031)
  blocking collectives: 55 us -> 64 us
    all_gather x0 -> x5, blocking collectives: none -> 50.6 us  [over_axes(): pieces = lax.all_gather(value, axis)]
    psum x5 -> x0, blocking collectives: 41.6 us -> none  [over_axes(): value = lax.psum(value, axis)]
where the time goes in v1:
time: 393 us
  waiting for transfers between devices  277 us (70%)
  blocking collectives  64 us (16%)
  matrix products  25.7 us (7%)
  between operations  13.9 us (4%)
  other arithmetic  6.07 us (2%)
  starting transfers between devices  4.29 us (1%)
    all_gather x1, waiting for transfers between devices, in_one_piece(): out = lax.all_gather(both, axis, axis=dim, tiled=True)  184 us
    reduce_scatter x3, waiting for transfers between devices, own_rows_2(): so_far = lax.psum_scatter(so_far, axis, scatter_dimension=0, tiled=True)  85.4 us
    all_gather x5, blocking collectives, over_axes(): pieces = lax.all_gather(value, axis)  50.6 us
    all_to_all x1, blocking collectives, sent_to_all(): lax.all_to_all(jnp.broadcast_to(value[None], (peers, *value.shape)), axis...  13.4 us
  transfers between devices with their start and end apart: 5, of which 4 were waited for; matrix products, arithmetic and copies ran while one was open for 4% of the time, Pallas kernels for 0%

profile of v1, /device:TPU:1, one launch (start us, length us, event | category | flops | bytes accessed | tf_op | source)
XLA Modules:
  0.0 392.6 jit_solution(2913457596314140396)
XLA Ops:
  7.2 0.0 all-gather.7.cloned.1.call-start
  7.2 1.7 pad_maximum_fusion
  8.9 0.0 all-gather.7.cloned.1.call-update
  8.9 0.0 copy-start.1
  8.9 0.0 reduce-scatter.4.cloned.1.call-start
  9.0 1.0 broadcast_in_dim.2
  10.0 13.4 %all_to_all.10 = bf16[4,32,2048]{2,1,0:T(8,128)(2,1)S(1)} all-to-all(bf16[4,32,2048]{2,1,0:T(8,128)(2,1)S(1)} %broadcast_in_dim.2), channel_id=1, replica_groups=mesh['seq_0'=4,'seq_1'=8,'seq_2'=2,'tp_0'=2,'tp_1'=2] {'tp_0','tp_1'}, dimensions={0} | all-to-all | bytes 1048576 | tf_op jit(solution)/shard_map/all_to_all | solution.py:14
  23.3 0.2 multiply_reduce_fusion
  23.5 0.1 rsqrt.20
  23.6 0.9 bitcast_multiply_fusion
  24.5 184.2 %all-gather.7.cloned.1.call-done = bf16[2048,3584]{1,0:T(8,128)(2,1)} async-done(((bf16[32,3584]{1,0:T(8,128)(2,1)}), bf16[2048,3584]{1,0:T(8,128)(2,1)}) %all-gather.7.cloned.1.call-update) | async-done | bytes 14680080 | tf_op jit(solution)/shard_map/all_gather | solution.py:33
  208.7 4.2 %fusion.2 = f32[128,1792]{1,0:T(8,128)S(1)} fusion(bf16[128,2048]{1,0:T(8,128)(2,1)S(1)} %get-tuple-element.6, bf16[2048,3584]{1,0:T(8,128)(2,1)} %all-gather.7.cloned.1.call-done), kind=kOutput, calls=%fused_computation.3 | convolution fusion | flops 939524096 | bytes 8781824 | tf_op jit(solution)/shard_map/dot_general | solution.py:70
  212.9 0.0 copy-done.1
  212.9 4.5 %fusion.23 = bf16[128,1792]{1,0:T(8,128)(2,1)S(1)} fusion(bf16[128,2048]{1,0:T(8,128)(2,1)S(1)} %get-tuple-element.6, bf16[2048,3584]{1,0:T(8,128)(2,1)} %all-gather.7.cloned.1.call-done, bf16[128,1792]{1,0:T(8,128)(2,1)S(1)} %copy-done.1, f32[128,1792]{1,0:T(8,128)S(1)} %fusion.2), kind=kOutput, calls=%fused_computation.14 | convolution fusion | flops 942047232 | bytes 9699328 | tf_op jit(solution)/shard_map/dot_general | solution.py:71
  217.4 5.0 %convolution_convert_fusion = bf16[2048,1792]{1,0:T(8,128)(2,1)} fusion(bf16[128,2048]{1,0:T(8,128)(2,1)S(1)} %get-tuple-element.6, bf16[128,1792]{1,0:T(8,128)(2,1)S(1)} %fusion.23), kind=kOutput, calls=%fused_computation | convolution fusion | flops 943194112 | bytes 8323072 | tf_op jit(solution)/shard_map/dot_general | solution.py:93
  222.5 0.0 reduce-scatter.4.cloned.1.call-update
  222.5 0.0 reduce-scatter.6.cloned.1.call-start
  222.5 72.7 %reduce-scatter.4.cloned.1.call-done = bf16[512,1792]{1,0:T(8,128)(2,1)} async-done(((bf16[2048,1792]{1,0:T(8,128)(2,1)}), bf16[512,1792]{1,0:T(8,128)(2,1)}) %reduce-scatter.4.cloned.1.call-update) | async-done | bytes 1835024 | tf_op jit(solution)/shard_map/reduce_scatter | solution.py:59
  295.2 0.0 reduce-scatter.6.cloned.1.call-update
  295.3 5.5 %fusion = f32[128,2048]{1,0:T(8,128)S(1)} fusion(bf16[128,1792]{1,0:T(8,128)(2,1)S(1)} %fusion.23, bf16[2048,3584]{1,0:T(8,128)(2,1)} %all-gather.7.cloned.1.call-done), kind=kOutput, calls=%fused_computation.1 | convolution fusion | flops 939524096 | bytes 8847360 | tf_op jit(solution)/shard_map/dot_general | solution.py:79
  300.8 0.0 copy-start
  300.8 6.4 %fusion.20 = bf16[128,2048]{1,0:T(8,128)(2,1)} fusion(f32[128,2048]{1,0:T(8,128)S(1)} %fusion, bf16[2048,3584]{1,0:T(8,128)(2,1)} %all-gather.7.cloned.1.call-done, f32[128,1792]{1,0:T(8,128)S(1)} %fusion.2, bf16[128,1792]{1,0:T(8,128)(2,1)S(1)} %copy-done.1), kind=kOutput, calls=%fused_computation.13 | convolution fusion | flops 941654016 | bytes 10289152 | tf_op jit(solution)/shard_map/dot_general | solution.py:80
  307.2 4.2 %all-to-all-start.1 = ((bf16[4,32,2048]{2,1,0:T(8,128)(2,1)}), bf16[4,32,2048]{2,1,0:T(8,128)(2,1)S(1)}, u32[]{:S(2)}, u32[]{:S(2)}) async-start(bf16[4,32,2048]{2,1,0:T(8,128)(2,1)} %bitcast.2), calls=%async_computation.1 | async-start | bytes 1048576 | tf_op jit(solution)/shard_map/all_to_all | solution.py:45
  311.4 0.0 reduce-scatter.8.cloned.1.call-start
  311.4 0.1 rsqrt.19
  311.5 0.1 dynamic-slice_bitcast_fusion
  311.5 7.7 %all-to-all-done.1 = bf16[4,32,2048]{2,1,0:T(8,128)(2,1)S(1)} async-done(((bf16[4,32,2048]{2,1,0:T(8,128)(2,1)}), bf16[4,32,2048]{2,1,0:T(8,128)(2,1)S(1)}, u32[]{:S(2)}, u32[]{:S(2)}) %all-to-all-start.1) | async-done | bytes 524320 | tf_op jit(solution)/shard_map/all_to_all | solution.py:45
  319.2 0.1 convert_reduce_fusion
  319.3 0.0 copy-done
  319.3 0.2 multiply_reduce_fusion.1
  319.5 9.7 %all-gather = f32[8192]{0:T(1024)S(1)} all-gather(f32[2048]{0:T(1024)S(1)} %get-tuple-element.3), channel_id=2, replica_groups=mesh['seq_0'=4,'seq_1'=8,'seq_2'=2,'tp_0'=2,'tp_1'=2] {'seq_0'}, dimensions={0}, use_global_device_ids=true | all-gather | bytes 40960 | tf_op jit(solution)/shard_map/all_gather | solution.py:51
  329.3 20.3 %all-gather.1 = f32[16384]{0:T(1024)S(1)} all-gather(f32[2048]{0:T(1024)S(1)} %reduce_sum.85), channel_id=3, replica_groups=mesh['seq_0'=4,'seq_1'=8,'seq_2'=2,'tp_0'=2,'tp_1'=2] {'seq_1'}, dimensions={0}, use_global_device_ids=true | all-gather | bytes 73728 | tf_op jit(solution)/shard_map/all_gather | solution.py:51
  349.6 4.7 %all-gather.2 = f32[4096]{0:T(1024)S(1)} all-gather(f32[2048]{0:T(1024)S(1)} %reduce_sum.86), channel_id=4, replica_groups=mesh['seq_0'=4,'seq_1'=8,'seq_2'=2,'tp_0'=2,'tp_1'=2] {'seq_2'}, dimensions={0}, use_global_device_ids=true | all-gather | bytes 24576 | tf_op jit(solution)/shard_map/all_gather | solution.py:51
  354.4 3.5 all-gather.3
  357.9 0.0 reduce-scatter.6.cloned.1.call-done
  357.9 0.0 reduce-scatter.8.cloned.1.call-update
  357.9 12.4 %all-gather.4 = f32[4096]{0:T(1024)S(1)} all-gather(f32[2048]{0:T(1024)S(1)} %reduce_sum.88), channel_id=6, replica_groups=mesh['seq_0'=4,'seq_1'=8,'seq_2'=2,'tp_0'=2,'tp_1'=2] {'tp_1'}, dimensions={0}, use_global_device_ids=true | all-gather | bytes 24576 | tf_op jit(solution)/shard_map/all_gather | solution.py:51
  370.4 0.6 reduce_sum.89
  371.0 0.8 multiply_convert_fusion.1
  371.7 12.7 %reduce-scatter.8.cloned.1.call-done = bf16[32,1792]{1,0:T(8,128)(2,1)} async-done(((bf16[64,1792]{1,0:T(8,128)(2,1)}), bf16[32,1792]{1,0:T(8,128)(2,1)}) %reduce-scatter.8.cloned.1.call-update) | async-done | bytes 114704 | tf_op jit(solution)/shard_map/reduce_scatter | solution.py:59
  384.4 1.6 convert_element_type.47
  (11 shorter events, 0.2 us)
Async XLA Ops:
  7.2 201.5 %all-gather.7.cloned.1.call-start = ((), (), s32[]{:S(2)}) async-start(), calls=%async_computation.5 | async-start | bytes 14909440 | tf_op jit(solution)/shard_map/all_gather | solution.py:33
  8.9 204.0 %copy-start.1 = (bf16[128,1792]{1,0:T(8,128)(2,1)S(1)}, bf16[128,1792]{1,0:T(8,128)(2,1)}, u32[]{:S(2)}) copy-start(bf16[128,1792]{1,0:T(8,128)(2,1)} %param.9) | copy-start | bytes 1376260
  8.9 286.3 %reduce-scatter.4.cloned.1.call-start = ((), (), s32[]{:S(2)}) async-start(), calls=%async_computation.6 | async-start | bytes 9175040 | tf_op jit(solution)/shard_map/reduce_scatter | solution.py:59
  222.5 135.4 %reduce-scatter.6.cloned.1.call-start = ((), (), s32[]{:S(2)}) async-start(), calls=%async_computation.7 | async-start | bytes 2064384 | tf_op jit(solution)/shard_map/reduce_scatter | solution.py:59
  300.8 18.5 %copy-start = (f32[2048]{0:T(1024)S(1)}, f32[2048]{0:T(1024)}, u32[]{:S(2)}) copy-start(f32[2048]{0:T(1024)} %param.6) | copy-start | bytes 24580
  307.2 12.0 %all-to-all-start.1 = ((bf16[4,32,2048]{2,1,0:T(8,128)(2,1)}), bf16[4,32,2048]{2,1,0:T(8,128)(2,1)S(1)}, u32[]{:S(2)}, u32[]{:S(2)}) async-start(bf16[4,32,2048]{2,1,0:T(8,128)(2,1)} %bitcast.2), calls=%async_computation.1 | async-start | bytes 1048576 | tf_op jit(solution)/shard_map/all_to_all | solution.py:45
  311.4 73.1 %reduce-scatter.8.cloned.1.call-start = ((), (), s32[]{:S(2)}) async-start(), calls=%async_computation.8 | async-start | bytes 344064 | tf_op jit(solution)/shard_map/reduce_scatter | solution.py:59
Sparse Core Ops, SparseCore 0:
  12.2 196.4 all-gather.6
  222.6 72.5 reduce-scatter.3
  297.8 37.3 reduce-scatter.5
  358.0 26.3 reduce-scatter.7
